TPU v7x, 32 devices: a whole 2x2x4 slice. The times are simulated.
32 devices in a mesh: outer: 2 (over core), dp: 4 (over z), tensor: 4 (over y, x).
Axes of the slice: x: 2, y: 2, z: 4, core: 2. Of those that a mesh axis runs over, the one named last changes fastest.
Arguments:
- attn: bfloat16 [2048, 8192], P(('outer', 'dp'), 'tensor'), may hold values from -6 to 6
- out_weight: bfloat16 [8192, 8192], P(None, 'tensor'), may hold values from -0.0625 to 0.0625
- resid: bfloat16 [2048, 8192], P(('outer', 'dp'), 'tensor'), may hold values from -8 to 8
- norm_gain: bfloat16 [8192], P('tensor'), may hold values from 0.5 to 1.5
- head: bfloat16 [8192], P('tensor'), may hold values from -1 to 1
- lengths: int32 [32], P(('outer', 'dp')), may hold values from 1 to 64
- pairs: int32 [32, 2], P(('outer', 'dp')), may hold values from 0 to 3, as said below
- pair_valid: int32 [32], P(('outer', 'dp')), may hold values from 0 to 1, as said below
- loss_scale: float32 [1], replicated, may hold values from 1024 to 8192
Outputs:
- loss: float32 [1], replicated
- grad_out_proj: float32 [8192, 8192], P(('outer', 'dp'), 'tensor')
- grad_gain: float32 [8192], P('tensor')
- grad_head: float32 [8192], P('tensor')
Inputs may be any that keep to these rules, and one draw needn't show every extreme that they name: `pairs`: in each pair the two numbers differ; the first pair of each replica is valid. `pair_valid`: the first of each replica's 4 entries is 1.
All inputs are finite; a program needn't handle non-finite values.
Results may differ from a plain program's by a relative error of at most 0.003.
Values may be sent and summed in bfloat16 or wider, within the bound.
A program may use at most 128 MiB of HBM per device.

v0:
```python
import jax
import jax.numpy as jnp
from jax import lax
from jax.sharding import PartitionSpec as P


def shards(attn, out_weight, resid, norm_gain, head, lengths, pairs, pair_valid, loss_scale):
    f32 = jnp.float32
    tok_dev = attn.shape[0]
    feats = resid.shape[1]
    width = feats * lax.axis_size("tensor")
    seqs_dev = lengths.shape[0]
    seq_len = tok_dev // seqs_dev
    valid = pair_valid.astype(f32)
    proj = lax.psum_scatter(
        lax.dot_general(out_weight, attn, (((1,), (1,)), ((), ())), preferred_element_type=f32),
        "tensor",
        scatter_dimension=0,
        tiled=True,
    )
    z = resid.astype(f32).T + proj
    gain = norm_gain.astype(f32)[:, None]
    headv = head.astype(f32)[:, None]
    squares = lax.psum(jnp.sum(z * z, axis=0), "tensor")
    inv = 1.0 / jnp.sqrt(squares / width + 1e-05)
    normed = z * inv[None, :] * gain
    partial_score = jnp.sum(normed * headv, axis=0)
    position = jnp.arange(tok_dev)
    seq_of = position // seq_len
    within = position % seq_len
    member = (within[:, None] < lengths[None, :]) & (
        seq_of[:, None] == jnp.arange(seqs_dev)[None, :]
    )
    pooling = member.astype(f32) / lengths.astype(f32)[None, :]
    reward = lax.psum(jnp.sum(pooling * partial_score[:, None], axis=0), "tensor")
    choose = jnp.arange(seqs_dev)[None, :]
    select = (pairs[:, 0:1] == choose).astype(f32) - (pairs[:, 1:2] == choose).astype(f32)
    margin = jnp.sum(select * reward[None, :], axis=1)
    loss_part = jnp.sum(valid * jax.nn.softplus(-margin))
    loss_sum, count = lax.psum((loss_part, jnp.sum(valid)), ("outer", "dp"))
    dmargin = -loss_scale[0] * valid * jax.nn.sigmoid(-margin) / count
    dreward = jnp.sum(dmargin[:, None] * select, axis=0)
    dscore = jnp.sum(pooling * dreward[None, :], axis=1)
    head_part = jnp.sum(normed * dscore[None, :], axis=1)
    gain_part = jnp.sum(headv * z * (inv * dscore)[None, :], axis=1)
    scaled = dscore[None, :] * headv * gain
    inner = lax.psum(jnp.sum(scaled * z, axis=0), "tensor")
    dproj = inv[None, :] * scaled - z * (inv**3 * inner / width)[None, :]
    dproj = dproj.astype(jnp.bfloat16)
    gathered = lax.all_gather(dproj, "tensor", axis=0, tiled=True)
    exchanged = lax.all_to_all(gathered, ("outer", "dp"), split_axis=0, concat_axis=1, tiled=True)
    grad_out_proj = jnp.dot(
        exchanged,
        lax.all_gather(attn, ("outer", "dp"), axis=0, tiled=True),
        preferred_element_type=f32,
    )
    grad_gain, grad_head = lax.psum((gain_part, head_part), ("outer", "dp"))
    loss = (loss_sum / count).reshape(1)
    return (loss, grad_out_proj, grad_gain, grad_head)


def solution(mesh):
    return jax.shard_map(
        shards,
        mesh=mesh,
        in_specs=(
            P(("outer", "dp"), "tensor"),
            P(None, "tensor"),
            P(("outer", "dp"), "tensor"),
            P("tensor"),
            P("tensor"),
            P(("outer", "dp")),
            P(("outer", "dp"), None),
            P(("outer", "dp")),
            P(),
        ),
        out_specs=(P(), P(("outer", "dp"), "tensor"), P("tensor"), P("tensor")),
        check_vma=False,
    )
```

profile of v0, /device:TPU:6, one launch (start us, length us, event | category | flops | bytes accessed | tf_op | source)
XLA Modules:
  0.0 429.5 jit_solution(13942249505769072110)
XLA Ops:
  7.2 17.5 %fusion.8 = f32[8192,256]{1,0:T(8,128)} fusion(bf16[8192,2048]{1,0:T(8,128)(2,1)} %param.10, bf16[256,2048]{1,0:T(8,128)(2,1)} %param.9), kind=kOutput, calls=%fused_computation.38 | convolution fusion | flops 8589934592 | bytes 42991616 | tf_op jit(solution)/shard_map/dot_general | solution.py:16
  25.6 0.4 copy-done
  26.0 0.5 copy.16
  26.5 84.9 %reduce-scatter.2.cloned.1.call-done = f32[2048,256]{1,0:T(8,128)} async-done(((f32[8192,256]{1,0:T(8,128)}), f32[2048,256]{1,0:T(8,128)}) %reduce-scatter.2.cloned.1.call-update) | async-done | bytes 2097168 | tf_op jit(solution)/shard_map/reduce_scatter | solution.py:15
  111.4 2.0 multiply_reduce_fusion.4
  113.4 8.9 %psum.49 = f32[256]{0:T(256)S(1)} all-reduce(f32[256]{0:T(256)S(1)} %get-tuple-element.12), channel_id=1, replica_groups=mesh['outer'=2,'dp'=4,'tensor'=4] {'tensor'}, use_global_device_ids=true, to_apply=%region_2.0 | all-reduce | flops 256 | bytes 2048 | tf_op jit(solution)/shard_map/psum | solution.py:24
  122.3 0.7 multiply_reduce_fusion.3
  123.0 0.2 multiply_reduce_fusion.6
  123.2 8.9 %psum.50 = f32[4]{0:T(128)S(1)} all-reduce(f32[4]{0:T(128)S(1)} %multiply_reduce_fusion.6), channel_id=1, replica_groups=mesh['outer'=2,'dp'=4,'tensor'=4] {'tensor'}, use_global_device_ids=true, to_apply=%region_5.6 | all-reduce | flops 4 | bytes 32 | tf_op jit(solution)/shard_map/psum | solution.py:35
  132.1 0.2 multiply_reduce_fusion.8
  132.3 0.6 convert_reduce_fusion
  133.0 15.8 %psum.52 = f32[]{:T(128)} all-reduce(f32[]{:T(128)} %get-tuple-element.7), channel_id=1, replica_groups=mesh['outer'=2,'dp'=4,'tensor'=4] {'outer','dp'}, use_global_device_ids=true, to_apply=%region_10.11 | all-reduce | flops 1 | bytes 8 | tf_op jit(solution)/shard_map/psum | solution.py:40
  148.8 0.7 fusion.6
  149.4 0.1 multiply_reduce_fusion.7
  149.5 0.1 multiply_reduce_fusion.5
  149.6 1.4 multiply_reduce_fusion
  151.0 8.0 %psum.53 = f32[256]{0:T(256)S(1)} all-reduce(f32[256]{0:T(256)S(1)} %get-tuple-element.5), channel_id=1, replica_groups=mesh['outer'=2,'dp'=4,'tensor'=4] {'tensor'}, use_global_device_ids=true, to_apply=%region_14.15 | all-reduce | flops 256 | bytes 2048 | tf_op jit(solution)/shard_map/psum | solution.py:47
  159.1 1.5 subtract_convert_fusion
  160.6 0.7 all-gather.5.cloned.1.call-update
  161.3 50.5 %all-gather.3.cloned.1.call-done = bf16[8192,256]{1,0:T(8,128)(2,1)} async-done(((bf16[2048,256]{1,0:T(8,128)(2,1)}), bf16[8192,256]{1,0:T(8,128)(2,1)}) %all-gather.3.cloned.1.call-update) | async-done | bytes 4194320 | tf_op jit(solution)/shard_map/all_gather | solution.py:50
  211.9 6.4 %copy.17 = bf16[8,1024,256]{1,2,0:T(8,128)(2,1)} copy(bf16[8,1024,256]{2,1,0:T(8,128)(2,1)} %bitcast.17) | data formatting | bytes 8388608 | tf_op jit(solution)/shard_map/all_to_all | solution.py:51
  218.3 4.7 %all-to-all-start = ((bf16[8,1024,256]{1,2,0:T(8,128)(2,1)}), bf16[8,1024,256]{1,2,0:T(8,128)(2,1)}, u32[]{:S(2)}, u32[]{:S(2)}) async-start(bf16[8,1024,256]{1,2,0:T(8,128)(2,1)} %copy.17), calls=%async_computation.1 | async-start | bytes 8388608 | tf_op jit(solution)/shard_map/all_to_all | solution.py:51
  222.9 182.9 %all-reduce = (f32[]{:T(128)}, f32[2048]{0:T(1024)}, f32[2048]{0:T(1024)}) all-reduce(f32[]{:T(128)} %get-tuple-element.8, f32[2048]{0:T(1024)S(1)} %get-tuple-element.6, f32[2048]{0:T(1024)S(1)} %get-tuple-element.4), channel_id=1, replica_groups=mesh['outer'=2,'dp'=4,'tensor'=4] {'outer','dp'}, use_global_device_ids=true, to_apply=%region_8.9 | all-reduce | flops 4097 | bytes 32776 | tf_op jit(solution)/shard_map/psum | solution.py:40
  407.2 14.6 %fusion.9 = f32[1024,2048]{1,0:T(8,128)} fusion(bf16[1024,2048]{0,1:T(8,128)(2,1)} %bitcast.7, bf16[2048,2048]{1,0:T(8,128)(2,1)} %all-gather.5.cloned.1.call-done), kind=kOutput, calls=%fused_computation.39 | convolution fusion | flops 8589934592 | bytes 20971520 | tf_op jit(solution)/shard_map/dot_general | solution.py:52
  (26 shorter events, 0.3 us)
Async XLA Ops:
  7.2 104.3 %reduce-scatter.2.cloned.1.call-start = ((), (), s32[]{:S(2)}) async-start(), calls=%async_computation.2 | async-start | bytes 10485760 | tf_op jit(solution)/shard_map/reduce_scatter | solution.py:15
  24.7 0.8 copy-start.3
  24.7 0.9 copy-start.1
  24.7 0.9 copy-start.2
  24.7 1.3 copy-start
  24.7 1.8 copy-start.5
  24.7 187.1 %all-gather.3.cloned.1.call-start = ((), (), s32[]{:S(2)}) async-start(), calls=%async_computation.3 | async-start | bytes 5242880 | tf_op jit(solution)/shard_map/all_gather | solution.py:50
  113.4 18.9 %copy-start.4 = (s32[4]{0:T(128)S(1)}, s32[4]{0:T(128)}, u32[]{:S(2)}) copy-start(s32[4]{0:T(128)} %param.16) | copy-start | bytes 52
  160.6 246.6 %all-gather.5.cloned.1.call-start = ((), (), s32[]{:S(2)}) async-start(), calls=%async_computation.4 | async-start | bytes 9437184 | tf_op jit(solution)/shard_map/all_gather | solution.py:54
  218.3 188.9 %all-to-all-start = ((bf16[8,1024,256]{1,2,0:T(8,128)(2,1)}), bf16[8,1024,256]{1,2,0:T(8,128)(2,1)}, u32[]{:S(2)}, u32[]{:S(2)}) async-start(bf16[8,1024,256]{1,2,0:T(8,128)(2,1)} %copy.17), calls=%async_computation.1 | async-start | bytes 8388608 | tf_op jit(solution)/shard_map/all_to_all | solution.py:51
Sparse Core Ops, SparseCore 0:
  24.8 86.5 reduce-scatter.1
  160.7 51.1 all-gather.2
  213.5 161.4 all-gather.4
where the time goes:
time: 432 us; the launch traced here: 430 us
  blocking collectives  225 us (52%)
  waiting for transfers between devices  136 us (31%)
  matrix products  32.1 us (7%)
  between operations  17.1 us (4%)
  other arithmetic  7.44 us (2%)
  local copies, waits for them, and re-layouts  7.36 us (2%)
  starting transfers between devices  4.77 us (1%)
    psum x2, blocking collectives, shards(): loss_sum, count = lax.psum((loss_part, jnp.sum(valid)), ('outer', 'dp'))  199 us
    reduce_scatter x1, waiting for transfers between devices, shards(): lax.psum_scatter(lax.dot_general(out_weight, attn, (((1,), (1,)), ((), ()...  84.9 us
    all_gather x1, waiting for transfers between devices, shards(): gathered = lax.all_gather(dproj, 'tensor', axis=0, tiled=True)  50.5 us
    dot_general x1, matrix products, shards(): lax.dot_general(out_weight, attn, (((1,), (1,)), ((), ())), preferred_ele...  17.5 us
    dot_general x1, matrix products, shards(): jnp.dot(exchanged, lax.all_gather(attn, ('outer', 'dp'), axis=0, tiled=Tr...  14.6 us
    psum x1, blocking collectives, shards(): lax.psum(jnp.sum(pooling * partial_score[:, None], axis=0), 'tensor')  8.92 us
    psum x1, blocking collectives, shards(): squares = lax.psum(jnp.sum(z * z, axis=0), 'tensor')  8.91 us
  transfers between devices with their start and end apart: 4, of which 2 were waited for; matrix products, arithmetic and copies ran while one was open for 2% of the time, Pallas kernels for 0%

commit v1 on v0

v1 whole, which is shorter than its diff:
```python
import jax
import jax.numpy as jnp
from jax import lax
from jax.sharding import PartitionSpec as P


def shards(attn, out_weight, resid, norm_gain, head, lengths, pairs, pair_valid, loss_scale):
    f32 = jnp.float32
    tok_dev = attn.shape[0]
    feats = resid.shape[1]
    tensor = lax.axis_size("tensor")
    width = feats * tensor
    seqs_dev = lengths.shape[0]
    seq_len = tok_dev // seqs_dev
    valid = pair_valid.astype(f32)
    count = lax.psum(jnp.sum(valid), ("outer", "dp"))
    part = lax.dot_general(out_weight, attn, (((1,), (1,)), ((), ())), preferred_element_type=f32)
    part = part.astype(jnp.bfloat16).reshape(tensor, feats, tok_dev)
    part = lax.all_to_all(part, "tensor", split_axis=0, concat_axis=0, tiled=True)
    z = resid.astype(f32).T + jnp.sum(part.astype(f32), axis=0)
    gain = norm_gain.astype(f32)[:, None]
    headv = head.astype(f32)[:, None]
    both = headv * gain
    sums = lax.psum(jnp.stack([jnp.sum(z * z, axis=0), jnp.sum(z * both, axis=0)]), "tensor")
    inv = 1.0 / jnp.sqrt(sums[0] / width + 1e-05)
    score = sums[1] * inv
    position = jnp.arange(tok_dev)
    seq_of = position // seq_len
    within = position % seq_len
    member = (within[:, None] < lengths[None, :]) & (
        seq_of[:, None] == jnp.arange(seqs_dev)[None, :]
    )
    pooling = member.astype(f32) / lengths.astype(f32)[None, :]
    reward = jnp.sum(pooling * score[:, None], axis=0)
    choose = jnp.arange(seqs_dev)[None, :]
    select = (pairs[:, 0:1] == choose).astype(f32) - (pairs[:, 1:2] == choose).astype(f32)
    margin = jnp.sum(select * reward[None, :], axis=1)
    loss_part = jnp.sum(valid * jax.nn.softplus(-margin))
    dmargin = -loss_scale[0] * valid * jax.nn.sigmoid(-margin) / count
    dreward = jnp.sum(dmargin[:, None] * select, axis=0)
    dscore = jnp.sum(pooling * dreward[None, :], axis=1)
    weight = inv * dscore
    dproj = weight[None, :] * both - z * (inv**3 * dscore * sums[1] / width)[None, :]
    dproj = dproj.astype(jnp.bfloat16)
    zsum = jnp.sum(z * weight[None, :], axis=1)
    gathered = lax.all_gather(dproj, "tensor", axis=0, tiled=True)
    exchanged = lax.all_to_all(gathered, ("outer", "dp"), split_axis=0, concat_axis=1, tiled=True)
    grad_out_proj = jnp.dot(
        exchanged,
        lax.all_gather(attn, ("outer", "dp"), axis=0, tiled=True),
        preferred_element_type=f32,
    )
    zsum, loss_sum = lax.psum((zsum, loss_part), ("outer", "dp"))
    loss = (loss_sum / count).reshape(1)
    return (loss, grad_out_proj, zsum * headv[:, 0], zsum * gain[:, 0])


def solution(mesh):
    return jax.shard_map(
        shards,
        mesh=mesh,
        in_specs=(
            P(("outer", "dp"), "tensor"),
            P(None, "tensor"),
            P(("outer", "dp"), "tensor"),
            P("tensor"),
            P("tensor"),
            P(("outer", "dp")),
            P(("outer", "dp"), None),
            P(("outer", "dp")),
            P(),
        ),
        out_specs=(P(), P(("outer", "dp"), "tensor"), P("tensor"), P("tensor")),
        check_vma=False,
    )
```

time: 432 us -> 369 us (0.85)
  waiting for transfers between devices: 136 us -> 96.7 us
  blocking collectives: 225 us -> 197 us
  starting transfers between devices: 4.77 us -> 9.67 us
    reduce_scatter x1 -> x0, waiting for transfers between devices: 84.9 us -> none  [shards(): lax.psum_scatter(lax.dot_general(out_weight, attn, (((1,), (1,)), ((), ()...]
    all_to_all x0 -> x1, waiting for transfers between devices: none -> 45.2 us  [shards(): lax.all_to_all(part, 'tensor', split_axis=0, concat_axis=0, tiled=True)]
    psum x5 -> x3, blocking collectives: 225 us -> 197 us  [the longest x1 172 us: shards(): zsum, loss_sum = lax.psum((zsum, loss_part), ('outer', 'dp'))]
    all_to_all x0 -> x1, starting transfers between devices: none -> 4.98 us  [shards(): lax.all_to_all(part, 'tensor', split_axis=0, concat_axis=0, tiled=True)]
where the time goes in v1:
time: 369 us; the launch traced here: 366 us
  blocking collectives  197 us (53%)
  waiting for transfers between devices  96.7 us (26%)
  matrix products  31.4 us (9%)
  between operations  17.3 us (5%)
  starting transfers between devices  9.67 us (3%)
  other arithmetic  7.44 us (2%)
  local copies, waits for them, and re-layouts  7.02 us (2%)
    psum x1, blocking collectives, shards(): zsum, loss_sum = lax.psum((zsum, loss_part), ('outer', 'dp'))  172 us
    all_gather x1, waiting for transfers between devices, shards(): gathered = lax.all_gather(dproj, 'tensor', axis=0, tiled=True)  50.8 us
    all_to_all x1, waiting for transfers between devices, shards(): lax.all_to_all(part, 'tensor', split_axis=0, concat_axis=0, tiled=True)  45.2 us
    dot_general x1, matrix products, shards(): lax.dot_general(out_weight, attn, (((1,), (1,)), ((), ())), preferred_ele...  16.8 us
    psum x1, blocking collectives, shards(): count = lax.psum(jnp.sum(valid), ('outer', 'dp'))  16.2 us
    dot_general x1, matrix products, shards(): jnp.dot(exchanged, lax.all_gather(attn, ('outer', 'dp'), axis=0, tiled=Tr...  14.6 us
    psum x1, blocking collectives, shards(): lax.psum(jnp.stack([jnp.sum(z * z, axis=0), jnp.sum(z * both, axis=0)]),...  8.91 us
  transfers between devices with their start and end apart: 4, of which 2 were waited for; matrix products, arithmetic and copies ran while one was open for 2% of the time, Pallas kernels for 0%

profile of v1, /device:TPU:6, one launch (start us, length us, event | category | flops | bytes accessed | tf_op | source)
XLA Modules:
  0.0 366.3 jit_solution(16129040595212171715)
XLA Ops:
  7.2 16.8 %convolution_convert_fusion = bf16[8192,256]{1,0:T(8,128)(2,1)} fusion(bf16[8192,2048]{1,0:T(8,128)(2,1)} %param.10, bf16[256,2048]{1,0:T(8,128)(2,1)} %param.9), kind=kOutput, calls=%fused_computation | convolution fusion | flops 8592031744 | bytes 38797312 | tf_op jit(solution)/shard_map/dot_general | solution.py:17
  24.0 5.0 %all-to-all-start = ((bf16[4,2048,256]{2,1,0:T(8,128)(2,1)}), bf16[4,2048,256]{2,1,0:T(8,128)(2,1)}, u32[]{:S(2)}, u32[]{:S(2)}) async-start(bf16[4,2048,256]{2,1,0:T(8,128)(2,1)} %bitcast.31), calls=%async_computation | async-start | bytes 8388608 | tf_op jit(solution)/shard_map/all_to_all | solution.py:19
  28.9 0.0 all-gather.3.cloned.1.call-start
  29.0 0.5 copy.15
  30.3 45.2 %all-to-all-done = bf16[4,2048,256]{2,1,0:T(8,128)(2,1)} async-done(((bf16[4,2048,256]{2,1,0:T(8,128)(2,1)}), bf16[4,2048,256]{2,1,0:T(8,128)(2,1)}, u32[]{:S(2)}, u32[]{:S(2)}) %all-to-all-start) | async-done | bytes 4194336 | tf_op jit(solution)/shard_map/all_to_all | solution.py:19
  75.4 3.0 convert_reduce_fusion
  78.5 0.5 multiply_reduce_fusion.2
  78.9 8.9 %psum.28 = f32[2,256]{1,0:T(2,128)S(1)} all-reduce(f32[2,256]{1,0:T(2,128)S(1)} %pad_maximum_fusion), channel_id=1, replica_groups=mesh['outer'=2,'dp'=4,'tensor'=4] {'tensor'}, use_global_device_ids=true, to_apply=%region_3.0 | all-reduce | flops 512 | bytes 4096 | tf_op jit(solution)/shard_map/psum | solution.py:24
  87.9 0.2 multiply_reduce_fusion.4
  88.0 0.2 multiply_reduce_fusion.6
  88.2 0.6 convert_reduce_fusion.1
  88.9 16.2 %psum.30 = f32[]{:T(128)} all-reduce(f32[]{:T(128)} %get-tuple-element.6), channel_id=1, replica_groups=mesh['outer'=2,'dp'=4,'tensor'=4] {'outer','dp'}, use_global_device_ids=true, to_apply=%region_9.10 | all-reduce | flops 1 | bytes 8 | tf_op jit(solution)/shard_map/psum | solution.py:16
  105.1 0.7 fusion.9
  105.8 0.1 multiply_reduce_fusion.5
  105.8 0.1 multiply_reduce_fusion.3
  106.0 1.5 subtract_convert_fusion
  107.4 0.0 all-gather.5.cloned.1.call-start
  107.5 0.7 all-gather.5.cloned.1.call-update
  108.2 50.8 %all-gather.3.cloned.1.call-done = bf16[8192,256]{1,0:T(8,128)(2,1)} async-done(((bf16[2048,256]{1,0:T(8,128)(2,1)}), bf16[8192,256]{1,0:T(8,128)(2,1)}) %all-gather.3.cloned.1.call-update) | async-done | bytes 4194320 | tf_op jit(solution)/shard_map/all_gather | solution.py:46
  159.0 4.6 %all-to-all-start.1 = ((bf16[8,1024,256]{2,1,0:T(8,128)(2,1)}), bf16[8,1024,256]{2,1,0:T(8,128)(2,1)}, u32[]{:S(2)}, u32[]{:S(2)}) async-start(bf16[8,1024,256]{2,1,0:T(8,128)(2,1)} %bitcast.30), calls=%async_computation.1 | async-start | bytes 8388608 | tf_op jit(solution)/shard_map/all_to_all | solution.py:47
  163.6 171.7 %all-reduce = (f32[]{:T(128)}, f32[2048]{0:T(1024)S(1)}) all-reduce(f32[]{:T(128)} %get-tuple-element.7, f32[2048]{0:T(1024)S(1)} %get-tuple-element.11), channel_id=1, replica_groups=mesh['outer'=2,'dp'=4,'tensor'=4] {'outer','dp'}, use_global_device_ids=true, to_apply=%region_7.8 | all-reduce | flops 2049 | bytes 16392 | tf_op jit(solution)/shard_map/psum | solution.py:53
  336.6 0.6 convert_multiply_fusion
  337.3 6.5 %copy.16 = bf16[1024,8,256]{0,2,1:T(8,128)(2,1)} copy(bf16[1024,8,256]{2,0,1:T(8,128)(2,1)} %bitcast.13) | data formatting | bytes 8388608 | tf_op jit(solution)/shard_map/all_to_all | solution.py:47
  343.7 14.6 %fusion.11 = f32[1024,2048]{1,0:T(8,128)} fusion(bf16[1024,2048]{0,1:T(8,128)(2,1)} %bitcast.32, bf16[2048,2048]{1,0:T(8,128)(2,1)} %all-gather.5.cloned.1.call-done), kind=kOutput, calls=%fused_computation.44 | convolution fusion | flops 8589934592 | bytes 20971520 | tf_op jit(solution)/shard_map/dot_general | solution.py:48
  (22 shorter events, 0.1 us)
Async XLA Ops:
  23.9 5.1 %copy-start = (bf16[256,2048]{1,0:T(8,128)(2,1)S(1)}, bf16[256,2048]{1,0:T(8,128)(2,1)}, u32[]{:S(2)}) copy-start(bf16[256,2048]{1,0:T(8,128)(2,1)} %param.11) | copy-start | bytes 3145732
  23.9 5.6 %copy-start.3 = (s32[4]{0:T(128)S(1)}, s32[4]{0:T(128)}, u32[]{:S(2)}) copy-start(s32[4]{0:T(128)} %param.14) | copy-start | bytes 52
  23.9 6.3 %copy-start.5 = (s32[4,2]{0,1:T(2,128)S(1)}, s32[4,2]{0,1:T(2,128)}, u32[]{:S(2)}) copy-start(s32[4,2]{0,1:T(2,128)} %param.15) | copy-start | bytes 100
  23.9 6.3 %copy-start.1 = (bf16[2048]{0:T(1024)(128)(2,1)S(1)}, bf16[2048]{0:T(1024)(128)(2,1)}, u32[]{:S(2)}) copy-start(bf16[2048]{0:T(1024)(128)(2,1)} %param.12) | copy-start | bytes 12292
  23.9 6.3 %copy-start.2 = (bf16[2048]{0:T(1024)(128)(2,1)S(1)}, bf16[2048]{0:T(1024)(128)(2,1)}, u32[]{:S(2)}) copy-start(bf16[2048]{0:T(1024)(128)(2,1)} %param.13) | copy-start | bytes 12292
  24.0 51.5 %all-to-all-start = ((bf16[4,2048,256]{2,1,0:T(8,128)(2,1)}), bf16[4,2048,256]{2,1,0:T(8,128)(2,1)}, u32[]{:S(2)}, u32[]{:S(2)}) async-start(bf16[4,2048,256]{2,1,0:T(8,128)(2,1)} %bitcast.31), calls=%async_computation | async-start | bytes 8388608 | tf_op jit(solution)/shard_map/all_to_all | solution.py:19
  28.9 130.1 %all-gather.3.cloned.1.call-start = ((), (), s32[]{:S(2)}) async-start(), calls=%async_computation.2 | async-start | bytes 5242880 | tf_op jit(solution)/shard_map/all_gather | solution.py:46
  30.3 58.0 %copy-start.4 = (s32[4]{0:T(128)S(1)}, s32[4]{0:T(128)}, u32[]{:S(2)}) copy-start(s32[4]{0:T(128)} %param.16) | copy-start | bytes 52
  107.4 236.3 %all-gather.5.cloned.1.call-start = ((), (), s32[]{:S(2)}) async-start(), calls=%async_computation.3 | async-start | bytes 9437184 | tf_op jit(solution)/shard_map/all_gather | solution.py:50
  159.0 178.2 %all-to-all-start.1 = ((bf16[8,1024,256]{2,1,0:T(8,128)(2,1)}), bf16[8,1024,256]{2,1,0:T(8,128)(2,1)}, u32[]{:S(2)}, u32[]{:S(2)}) async-start(bf16[8,1024,256]{2,1,0:T(8,128)(2,1)} %bitcast.30), calls=%async_computation.1 | async-start | bytes 8388608 | tf_op jit(solution)/shard_map/all_to_all | solution.py:47
Sparse Core Ops, SparseCore 0:
  107.6 51.4 all-gather.2
  160.6 161.7 all-gather.4

commit v2 on v1

v2 whole, which is shorter than its diff:
```python
import functools

import jax
import jax.numpy as jnp
from jax import lax
from jax.experimental import pallas as pl
from jax.experimental.pallas import tpu as pltpu
from jax.sharding import PartitionSpec as P

MESH = pl.DeviceIdType.MESH
F32 = jnp.float32
BF16 = jnp.bfloat16
SLOTS = 3


def bits_of(count):
    return count.bit_length() - 1


def flip(index, mask, bits):
    out = 0
    for j in range(bits):
        out = out + ((index // 2**j + mask // 2**j) % 2) * 2**j
    return out


def kernel(
    sizes,
    attn,
    weight,
    resid,
    both,
    pool,
    select,
    scaled_valid,
    valid,
    vsum,
    exch,
    attn_all,
    qtot,
    ltot,
    ctot,
    wbuf,
    attn_t,
    part,
    got,
    z,
    dp,
    stat,
    stat_in,
    cin,
    lsrc,
    lin,
    qsrc,
    qin,
    wsem,
    rs_send,
    rs_recv,
    st_send,
    st_recv,
    c_send,
    c_recv,
    l_send,
    l_recv,
    q_send,
    q_recv,
    ag_local,
    ag_right,
    ag_left,
    ag_out,
    ag_recv,
    z_send,
    b_send,
    e_recv,
):
    T, O, Z = sizes
    N = O * Z
    bits = bits_of(T)
    R = N // T
    tok, feats = resid.shape
    width = feats * T
    blk = width // N
    tile = wbuf.shape[1]
    per = feats // tile
    o, p, t = lax.axis_index("outer"), lax.axis_index("dp"), lax.axis_index("tensor")
    me = o * Z + p

    def replica(k):
        return (k // Z, k % Z, t)

    def tensor_peer(r):
        return (o, p, flip(t, r, bits))

    barrier = pltpu.get_barrier_semaphore()
    for r in range(1, T):
        pl.semaphore_signal(barrier, inc=1, device_id=tensor_peer(r), device_id_type=MESH)
    for d in range(1, N):
        pl.semaphore_signal(barrier, inc=1, device_id=replica((me + d) % N), device_id_type=MESH)

    def load(i):
        target = flip(t, T - 1 - i // per, bits)
        start = pl.multiple_of(target * feats + (i % per) * tile, tile)
        return pltpu.make_async_copy(
            weight.at[pl.ds(start, tile)], wbuf.at[i % SLOTS], wsem.at[i % SLOTS]
        )

    for i in range(min(SLOTS - 1, T * per)):
        load(i).start()

    def turn_attn(c, carry):
        cols = pl.ds(pl.multiple_of(c * 128, 128), 128)
        attn_t[cols, :] = attn[:, cols].astype(F32).T.astype(BF16)
        return carry

    lax.fori_loop(0, feats // 128, turn_attn, 0)
    pl.semaphore_wait(barrier, T - 1 + N - 1)

    def peer_copy(src, dst, send, recv, d):
        return pltpu.make_async_remote_copy(
            src_ref=src,
            dst_ref=dst.at[d],
            send_sem=send.at[d],
            recv_sem=recv.at[d],
            device_id=replica((me + d) % N),
            device_id_type=MESH,
        )

    def block_rows(outer, b):
        return pl.ds(pl.multiple_of((outer * Z + b) * tok, tok), tok)

    def ag_copy(src, b, send, where):
        return pltpu.make_async_remote_copy(
            src_ref=src,
            dst_ref=attn_all.at[block_rows(o, b)],
            send_sem=send,
            recv_sem=ag_recv.at[o, b],
            device_id=where,
            device_id_type=MESH,
        )

    def right_copy(s):
        b = (p + Z - s) % Z
        src = attn if s == 0 else attn_all.at[block_rows(o, b)]
        return ag_copy(src, b, ag_right.at[s], (o, (p + 1) % Z, t))

    def left_copy(s):
        b = (p + s) % Z
        src = attn if s == 0 else attn_all.at[block_rows(o, b)]
        return ag_copy(src, b, ag_left.at[s], (o, (p + Z - 1) % Z, t))

    def right_sends(s):
        return (p >= s) & (p < Z - 1)

    def left_sends(s):
        return (p + s < Z) & (p > 0)

    def out_copy(b, e, own=False):
        src = attn if own else attn_all.at[block_rows(o, b)]
        return ag_copy(src, b, ag_out.at[e, b], ((o + e) % O, p, t))

    def arrived(outer, b):
        rows = attn_all.at[block_rows(outer, b)]
        return pltpu.make_async_remote_copy(
            src_ref=rows,
            dst_ref=rows,
            send_sem=ag_out.at[0, 0],
            recv_sem=ag_recv.at[outer, b],
            device_id=(o, (p + 1) % Z, t),
            device_id_type=MESH,
        )

    def arrival(s):
        for ok, b in ((p - 1 - s >= 0, (p + Z - 1 - s) % Z), (p + 1 + s < Z, (p + 1 + s) % Z)):

            @pl.when(ok)
            def _():
                arrived(o, b).wait_recv()
                for e in range(1, O):
                    out_copy(b, e).start()

        if s + 1 < Z - 1:
            for ok, copy in ((right_sends(s + 1), right_copy), (left_sends(s + 1), left_copy)):

                @pl.when(ok)
                def _():
                    copy(s + 1).start()

    for ok, copy in ((right_sends(0), right_copy), (left_sends(0), left_copy)):

        @pl.when(ok)
        def _():
            copy(0).start()

    for e in range(1, O):
        out_copy(p, e, True).start()
    own_rows = pltpu.make_async_copy(attn, attn_all.at[block_rows(o, p)], ag_local)
    own_rows.start()
    for d in range(1, N):
        peer_copy(vsum, cin, c_send, c_recv, d).start()

    def rs_copy(r, j):
        return pltpu.make_async_remote_copy(
            src_ref=part.at[r, j],
            dst_ref=got.at[r, j],
            send_sem=rs_send.at[r, j],
            recv_sem=rs_recv.at[r, j],
            device_id=tensor_peer(r),
            device_id_type=MESH,
        )

    def project(i, carry):
        @pl.when(i + SLOTS - 1 < T * per)
        def _():
            load(i + SLOTS - 1).start()

        load(i).wait()
        r, j = T - 1 - i // per, i % per
        part[r, j] = jnp.dot(
            wbuf[i % SLOTS], attn_t[...], preferred_element_type=F32
        ).astype(BF16)

        @pl.when(r > 0)
        def _():
            rs_copy(r, j).start()

        return carry

    lax.fori_loop(0, T * per, project, 0)

    def rows_of(j):
        return pl.ds(pl.multiple_of(j * tile, tile), tile)

    def turn_resid(j, carry):
        z[rows_of(j), :] = resid[:, rows_of(j)].astype(F32).T + part[0, j].astype(F32)
        return carry

    lax.fori_loop(0, per, turn_resid, 0)
    arrival(0)

    def gather_z(j, carry):
        squares, heads = carry
        total = z[rows_of(j), :]
        for r in range(T - 1, 0, -1):
            rs_copy(r, j).wait_recv()
            total = total + got[r, j].astype(F32)
        z[rows_of(j), :] = total
        squares = squares + jnp.sum(total * total, axis=0, keepdims=True)
        heads = heads + jnp.sum(total * both[rows_of(j), :], axis=0, keepdims=True)
        return squares, heads

    zero = jnp.zeros((1, tok), F32)
    squares, heads = lax.fori_loop(0, per, gather_z, (zero, zero))
    stat[0:1, :] = squares
    stat[1:2, :] = heads

    def stat_copy(r):
        return pltpu.make_async_remote_copy(
            src_ref=stat,
            dst_ref=stat_in.at[r],
            send_sem=st_send.at[r],
            recv_sem=st_recv.at[r],
            device_id=tensor_peer(r),
            device_id_type=MESH,
        )

    for r in range(1, T):
        stat_copy(r).start()
    count = vsum[0:1, 0:1]
    for d in range(1, N):
        peer_copy(vsum, cin, c_send, c_recv, d).wait_recv()
        count = count + cin[d, 0:1, 0:1]
    if Z > 2:
        arrival(1)
    for r in range(1, T):
        stat_copy(r).wait_recv()
        squares = squares + stat_in[r, 0:1, :]
        heads = heads + stat_in[r, 1:2, :]
    inv = 1.0 / jnp.sqrt(squares / width + 1e-05)
    score = heads * inv
    reward = jnp.sum(pool[...] * score, axis=1, keepdims=True)
    margin = jnp.sum(select[...] * reward, axis=0, keepdims=True)
    soft = jnp.maximum(-margin, 0.0) + jnp.log1p(jnp.exp(-jnp.abs(margin)))
    loss = jnp.sum(valid[...] * soft, axis=1, keepdims=True)
    dmargin = scaled_valid[...] * jax.nn.sigmoid(-margin) / count
    dreward = jnp.sum(select[...] * dmargin, axis=1, keepdims=True)
    dscore = jnp.sum(pool[...] * dreward, axis=0, keepdims=True)
    scale = inv * dscore
    pull = inv * inv * inv * dscore * heads / width

    def make_dproj(j, carry):
        rows = rows_of(j)
        dp[rows, :] = (scale * both[rows, :] - z[rows, :] * pull).astype(BF16)
        return carry

    lax.fori_loop(0, per, make_dproj, 0)

    def cols_of(k):
        return exch.at[:, pl.ds(pl.multiple_of(k * tok, tok), tok)]

    def piece(j):
        return dp.at[pl.ds(j * blk, blk)]

    def piece_copy(j):
        return pltpu.make_async_remote_copy(
            src_ref=piece(j),
            dst_ref=cols_of(me),
            send_sem=z_send.at[j],
            recv_sem=e_recv.at[me],
            device_id=replica(t * R + j),
            device_id_type=MESH,
        )

    def piece_local(j):
        return pltpu.make_async_copy(piece(j), cols_of(me), e_recv.at[me])

    for j in range(R):

        @pl.when(t * R + j != me)
        def _():
            piece_copy(j).start()

        @pl.when(t * R + j == me)
        def _():
            piece_local(j).start()

    lsrc[...] = jnp.broadcast_to(loss, lsrc.shape)
    for j in range(per):
        rows = pl.ds(j * tile, tile)
        zw = z[rows, :] * scale
        lanes = zw[:, 0:128]
        for h in range(1, tok // 128):
            lanes = lanes + zw[:, h * 128 : (h + 1) * 128]
        qsrc[0:1, j * tile : (j + 1) * tile] = jnp.sum(lanes.T, axis=0, keepdims=True)
    for d in range(1, N):
        peer_copy(lsrc, lin, l_send, l_recv, d).start()
        peer_copy(qsrc, qin, q_send, q_recv, d).start()

    owner = me // R
    rank = flip(t, owner, bits)
    step = 1 + (p // (Z - Z // 2)) * (Z - 2)

    def child_copy(j, k):
        return pltpu.make_async_remote_copy(
            src_ref=cols_of(k),
            dst_ref=cols_of(k),
            send_sem=b_send.at[j, k],
            recv_sem=e_recv.at[k],
            device_id=tensor_peer(2**j),
            device_id_type=MESH,
        )

    def spread(i, carry):
        k = ((o + i) % O) * Z + (p + step * (i // O)) % Z
        child_copy(0, k).wait_recv()
        for j in range(bits):

            @pl.when(rank < 2**j)
            def _():
                child_copy(j, k).start()

        return carry

    lax.fori_loop(0, N // 2, spread, 0)
    for s in range(2, Z - 1):
        arrival(s)
    lax.fori_loop(N // 2, N, spread, 0)
    if Z == 2:
        pass

    ltotal, qtotal = lsrc[...], qsrc[...]
    for d in range(1, N):
        peer_copy(lsrc, lin, l_send, l_recv, d).wait_recv()
        peer_copy(qsrc, qin, q_send, q_recv, d).wait_recv()
        ltotal = ltotal + lin[d]
        qtotal = qtotal + qin[d]
    ltot[...] = ltotal
    qtot[...] = qtotal
    ctot[...] = jnp.broadcast_to(count, ctot.shape)

    for e in range(1, O):
        for b in range(Z):
            arrived((o + e) % O, b).wait_recv()
    own_rows.wait()
    for s in range(Z - 1):
        for ok, copy in ((right_sends(s), right_copy), (left_sends(s), left_copy)):

            @pl.when(ok)
            def _():
                copy(s).wait_send()

    for e in range(1, O):
        for b in range(Z):
            out_copy(b, e).wait_send()
    for d in range(1, N):
        peer_copy(vsum, cin, c_send, c_recv, d).wait_send()
        peer_copy(lsrc, lin, l_send, l_recv, d).wait_send()
        peer_copy(qsrc, qin, q_send, q_recv, d).wait_send()
    for r in range(1, T):
        stat_copy(r).wait_send()
        for j in range(per):
            rs_copy(r, j).wait_send()
    for j in range(R):

        @pl.when(t * R + j != me)
        def _():
            piece_copy(j).wait_send()

    def spread_end(k, carry):
        for j in range(bits):

            @pl.when(rank < 2**j)
            def _():
                child_copy(j, k).wait_send()

        return carry

    lax.fori_loop(0, N, spread_end, 0)


def shards(sizes, attn, out_weight, resid, norm_gain, head, lengths, pairs, pair_valid, loss_scale):
    T, O, Z = sizes
    N = O * Z
    tok, feats = resid.shape
    width = feats * T
    blk = width // N
    heads_dev = attn.shape[1]
    tile = min(512, feats)
    per = feats // tile
    seqs_dev = lengths.shape[0]
    seq_len = tok // seqs_dev
    valid = pair_valid.astype(F32)
    gain = norm_gain.astype(F32)
    headv = head.astype(F32)
    position = jnp.arange(tok)[None, :]
    mine = jnp.arange(seqs_dev)[:, None]
    member = (position % seq_len < lengths[:, None]) & (position // seq_len == mine)
    pool = member.astype(F32) / lengths.astype(F32)[:, None]
    select = (pairs[:, 0][None, :] == mine).astype(F32) - (pairs[:, 1][None, :] == mine).astype(F32)
    vsum = jnp.broadcast_to(jnp.sum(valid), (8, 128))
    vmem = pl.BlockSpec(memory_space=pltpu.VMEM)
    anyw = pl.BlockSpec(memory_space=pl.ANY)
    sem = pltpu.SemaphoreType.DMA
    bits = bits_of(T)
    exch, attn_all, qtot, ltot, ctot = pl.pallas_call(
        functools.partial(kernel, sizes),
        out_shape=(
            jax.ShapeDtypeStruct((blk, N * tok), BF16),
            jax.ShapeDtypeStruct((N * tok, heads_dev), BF16),
            jax.ShapeDtypeStruct((1, feats), F32),
            jax.ShapeDtypeStruct((8, 128), F32),
            jax.ShapeDtypeStruct((8, 128), F32),
        ),
        in_specs=[vmem, anyw, vmem, vmem, vmem, vmem, vmem, vmem, vmem],
        out_specs=(anyw, anyw, vmem, vmem, vmem),
        scratch_shapes=[
            pltpu.VMEM((SLOTS, tile, heads_dev), BF16),
            pltpu.VMEM((heads_dev, tok), BF16),
            pltpu.VMEM((T, per, tile, tok), BF16),
            pltpu.VMEM((T, per, tile, tok), BF16),
            pltpu.VMEM((feats, tok), F32),
            pltpu.VMEM((feats, tok), BF16),
            pltpu.VMEM((2, tok), F32),
            pltpu.VMEM((T, 2, tok), F32),
            pltpu.VMEM((N, 8, 128), F32),
            pltpu.VMEM((8, 128), F32),
            pltpu.VMEM((N, 8, 128), F32),
            pltpu.VMEM((1, feats), F32),
            pltpu.VMEM((N, 1, feats), F32),
            sem((SLOTS,)),
            sem((T, per)),
            sem((T, per)),
            sem((T,)),
            sem((T,)),
            sem((N,)),
            sem((N,)),
            sem((N,)),
            sem((N,)),
            sem((N,)),
            sem((N,)),
            sem,
            sem((Z,)),
            sem((Z,)),
            sem((O, Z)),
            sem((O, Z)),
            sem((N // T,)),
            sem((bits, N)),
            sem((N,)),
        ],
        compiler_params=pltpu.CompilerParams(
            collective_id=0, has_side_effects=True, vmem_limit_bytes=60 * 1024 * 1024
        ),
    )(
        attn,
        out_weight,
        resid,
        (gain * headv)[:, None],
        pool,
        select,
        (-loss_scale[0] * valid)[None, :],
        valid[None, :],
        vsum,
    )
    grad_out_proj = jnp.dot(exch, attn_all, preferred_element_type=F32)
    loss = (ltot[0, 0] / ctot[0, 0]).reshape(1)
    return (loss, grad_out_proj, qtot[0] * headv, qtot[0] * gain)


def solution(mesh):
    sizes = (mesh.shape["tensor"], mesh.shape["outer"], mesh.shape["dp"])
    return jax.shard_map(
        functools.partial(shards, sizes),
        mesh=mesh,
        in_specs=(
            P(("outer", "dp"), "tensor"),
            P(None, "tensor"),
            P(("outer", "dp"), "tensor"),
            P("tensor"),
            P("tensor"),
            P(("outer", "dp")),
            P(("outer", "dp"), None),
            P(("outer", "dp")),
            P(),
        ),
        out_specs=(P(), P(("outer", "dp"), "tensor"), P("tensor"), P("tensor")),
        check_vma=False,
    )
```

time: 369 us -> 191 us (0.52)
  blocking collectives: 197 us -> 0 us
  Pallas kernels: 0 us -> 160 us
  waiting for transfers between devices: 96.7 us -> 0 us
  matrix products: 31.4 us -> 14.5 us
  between operations: 17.3 us -> 3.79 us
  starting transfers between devices: 9.67 us -> 0 us
    psum x3 -> x0, blocking collectives: 197 us -> none  [the longest x1 172 us: shards(): zsum, loss_sum = lax.psum((zsum, loss_part), ('outer', 'dp'))]
    pallas_call x0 -> x1, Pallas kernels: none -> 160 us  [shards(): pl.pallas_call(functools.partial(kernel, sizes), out_shape=(jax.ShapeDtyp...]
    all_gather x2 -> x0, waiting for transfers between devices: 50.8 us -> none  [the longest x1 50.8 us: shards(): gathered = lax.all_gather(dproj, 'tensor', axis=0, tiled=True)]
    all_to_all x2 -> x0, waiting for transfers between devices: 45.2 us -> none  [the longest x1 45.2 us: shards(): lax.all_to_all(part, 'tensor', split_axis=0, concat_axis=0, tiled=True)]
    dot_general x2 -> x1, matrix products: 31.4 us -> 14.5 us  [shards(): grad_out_proj = jnp.dot(exch, attn_all, preferred_element_type=F32)]
    all_to_all x2 -> x0, starting transfers between devices: 9.59 us -> none  [the longest x1 4.98 us: shards(): lax.all_to_all(part, 'tensor', split_axis=0, concat_axis=0, tiled=True)]
    all_to_all x1 -> x0, local copies, waits for them, and re-layouts: 6.46 us -> none  [shards(): lax.all_to_all(gathered, ('outer', 'dp'), split_axis=0, concat_axis=1, ti...]
  transfers between devices with their start and end apart: 4 -> 0, of which waited for: 2 -> 0; matrix products, arithmetic and copies ran while one was open for 2% -> 0% of each run, Pallas kernels for 0% -> 0%
where the time goes in v2:
time: 191 us
  Pallas kernels  160 us (84%)
  matrix products  14.5 us (8%)
  other arithmetic  6.84 us (4%)
  local copies, waits for them, and re-layouts  5.66 us (3%)
  between operations  3.79 us (2%)
    pallas_call x1, Pallas kernels, shards(): pl.pallas_call(functools.partial(kernel, sizes), out_shape=(jax.ShapeDtyp...  160 us
    dot_general x1, matrix products, shards(): grad_out_proj = jnp.dot(exch, attn_all, preferred_element_type=F32)  14.5 us

profile of v2, /device:TPU:6, one launch (start us, length us, event | category | flops | bytes accessed | tf_op | source)
XLA Modules:
  0.0 191.1 jit_solution(15935631188361479190)
XLA Ops:
  0.6 0.7 convert_multiply_fusion.1
  1.3 1.3 copy.13.both
  2.7 0.7 convert_element_type.24
  3.3 1.3 convert_divide_fusion.pool
  4.7 0.8 slice_bitcast_fusion.1
  5.4 0.6 convert_subtract_fusion.select
  6.7 1.8 convert_reduce_fusion
  8.5 1.2 convert_bitcast_fusion.valid
  9.6 1.2 broadcast_in_dim.19.vsum
  10.8 160.3 %shard_map.120 = (bf16[1024,2048]{1,0:T(8,128)(2,1)}, bf16[2048,2048]{1,0:T(8,128)(2,1)}, f32[1,2048]{1,0:T(1,128)}, f32[8,128]{1,0:T(8,128)}, f32[8,128]{1,0:T(8,128)}) custom-call(bf16[256,2048]{1,0:T(8,128)(2,1)} %attn.1, bf16[8192,2048]{1,0:T(8,128)(2,1)} %weight.1, bf16[256,2048]{1,0:T(8,128)(2,1)} %resid.1, f32[2048,1]{1,0:T(8,128)} %copy.13.both, ...), custom_call_target="tpu_custom_call" | custom-call | tf_op jit(solution)/shard_map/pallas_call | solution.py:444
  171.1 1.2 slice.14
  172.3 1.2 slice.15
  174.8 0.0 copy-start
  174.8 0.0 copy-start.1
  174.8 0.0 copy-start.2
  174.8 14.5 %fusion.2 = f32[1024,2048]{1,0:T(8,128)} fusion(bf16[1024,2048]{1,0:T(8,128)(2,1)} %get-tuple-element.11, bf16[2048,2048]{1,0:T(8,128)(2,1)} %get-tuple-element.12), kind=kOutput, calls=%fused_computation.20 | convolution fusion | flops 8589934592 | bytes 20971520 | tf_op jit(solution)/shard_map/dot_general | solution.py:503
  189.3 0.0 copy-done
  189.3 0.0 copy-done.1
  189.3 0.0 copy-done.2
  189.3 0.6 convert_multiply_fusion.2
  (1 shorter events, 0.0 us)
Async XLA Ops:
  174.8 14.5 %copy-start = (bf16[2048]{0:T(1024)(128)(2,1)S(1)}, bf16[2048]{0:T(1024)(128)(2,1)}, u32[]{:S(2)}) copy-start(bf16[2048]{0:T(1024)(128)(2,1)} %param.13) | copy-start | bytes 12292
  174.8 14.5 %copy-start.1 = (bf16[2048]{0:T(1024)(128)(2,1)S(1)}, bf16[2048]{0:T(1024)(128)(2,1)}, u32[]{:S(2)}) copy-start(bf16[2048]{0:T(1024)(128)(2,1)} %param.12) | copy-start | bytes 12292
  174.8 14.5 %copy-start.2 = (f32[1,2048]{1,0:T(1,128)S(1)}, f32[1,2048]{1,0:T(1,128)}, u32[]{:S(2)}) copy-start(f32[1,2048]{1,0:T(1,128)} %get-tuple-element.13) | copy-start | bytes 24580

commit v3 on v2

--- a/solution.py
+++ b/solution.py
@@ -35,11 +35,13 @@
     scaled_valid,
     valid,
     vsum,
-    exch,
-    attn_all,
+    grad,
     qtot,
     ltot,
     ctot,
+    exch,
+    attn_all,
+    acc,
     wbuf,
     attn_t,
     part,
@@ -72,6 +74,7 @@
     z_send,
     b_send,
     e_recv,
+    o_sem,
 ):
     T, O, Z = sizes
     N = O * Z
@@ -126,7 +129,7 @@
         )
 
     def block_rows(outer, b):
-        return pl.ds(pl.multiple_of((outer * Z + b) * tok, tok), tok)
+        return outer * Z + b
 
     def ag_copy(src, b, send, where):
         return pltpu.make_async_remote_copy(
@@ -235,6 +238,12 @@
         return carry
 
     lax.fori_loop(0, per, turn_resid, 0)
+
+    def clear(j, carry):
+        acc[pl.ds(pl.multiple_of(j * 128, 128), 128), :] = jnp.zeros((128, acc.shape[1]), F32)
+        return carry
+
+    lax.fori_loop(0, blk // 128, clear, 0)
     arrival(0)
 
     def gather_z(j, carry):
@@ -295,7 +304,7 @@
     lax.fori_loop(0, per, make_dproj, 0)
 
     def cols_of(k):
-        return exch.at[:, pl.ds(pl.multiple_of(k * tok, tok), tok)]
+        return exch.at[k]
 
     def piece(j):
         return dp.at[pl.ds(j * blk, blk)]
@@ -349,8 +358,12 @@
             device_id_type=MESH,
         )
 
-    def spread(i, carry):
-        k = ((o + i) % O) * Z + (p + step * (i // O)) % Z
+    def place(i):
+        return (o + i) % O, (p + step * (i // O)) % Z
+
+    def forward(i):
+        outer, b = place(i)
+        k = outer * Z + b
         child_copy(0, k).wait_recv()
         for j in range(bits):
 
@@ -358,14 +371,54 @@
             def _():
                 child_copy(j, k).start()
 
-        return carry
-
-    lax.fori_loop(0, N // 2, spread, 0)
+    wide = min(512, acc.shape[1])
+    strips = acc.shape[1] // wide
+
+    def strip(c):
+        return pl.ds(pl.multiple_of(c * wide, wide), wide)
+
+    def out_strip(c):
+        return pltpu.make_async_copy(acc.at[:, strip(c)], grad.at[:, strip(c)], o_sem.at[c])
+
+    def multiply(i):
+        outer, b = place(i)
+        k = outer * Z + b
+
+        @pl.when(i % O > 0)
+        def _():
+            arrived(outer, b).wait_recv()
+
+        def one(c, carry):
+            acc[:, strip(c)] += jnp.dot(
+                exch[k], attn_all[k, :, strip(c)], preferred_element_type=F32
+            )
+
+            @pl.when(i == N - 1)
+            def _():
+                out_strip(c).start()
+
+            return carry
+
+        lax.fori_loop(0, strips, one, 0)
+
+    def first_half(i, carry):
+        forward(i)
+        return carry
+
+    def second_half(i, carry):
+        forward(i)
+
+        def both_halves(h, inner):
+            multiply(i - N // 2 + h * (N // 2))
+            return inner
+
+        return lax.fori_loop(0, 2, both_halves, carry)
+
+    own_rows.wait()
+    lax.fori_loop(0, N // 2, first_half, 0)
     for s in range(2, Z - 1):
         arrival(s)
-    lax.fori_loop(N // 2, N, spread, 0)
-    if Z == 2:
-        pass
+    lax.fori_loop(N // 2, N, second_half, 0)
 
     ltotal, qtotal = lsrc[...], qsrc[...]
     for d in range(1, N):
@@ -377,10 +430,6 @@
     qtot[...] = qtotal
     ctot[...] = jnp.broadcast_to(count, ctot.shape)
 
-    for e in range(1, O):
-        for b in range(Z):
-            arrived((o + e) % O, b).wait_recv()
-    own_rows.wait()
     for s in range(Z - 1):
         for ok, copy in ((right_sends(s), right_copy), (left_sends(s), left_copy)):
 
@@ -415,6 +464,8 @@
         return carry
 
     lax.fori_loop(0, N, spread_end, 0)
+    for c in range(strips):
+        out_strip(c).wait()
 
 
 def shards(sizes, attn, out_weight, resid, norm_gain, head, lengths, pairs, pair_valid, loss_scale):
@@ -441,18 +492,20 @@
     anyw = pl.BlockSpec(memory_space=pl.ANY)
     sem = pltpu.SemaphoreType.DMA
     bits = bits_of(T)
-    exch, attn_all, qtot, ltot, ctot = pl.pallas_call(
+    grad_out_proj, qtot, ltot, ctot = pl.pallas_call(
         functools.partial(kernel, sizes),
         out_shape=(
-            jax.ShapeDtypeStruct((blk, N * tok), BF16),
-            jax.ShapeDtypeStruct((N * tok, heads_dev), BF16),
+            jax.ShapeDtypeStruct((blk, heads_dev), F32),
             jax.ShapeDtypeStruct((1, feats), F32),
             jax.ShapeDtypeStruct((8, 128), F32),
             jax.ShapeDtypeStruct((8, 128), F32),
         ),
         in_specs=[vmem, anyw, vmem, vmem, vmem, vmem, vmem, vmem, vmem],
-        out_specs=(anyw, anyw, vmem, vmem, vmem),
+        out_specs=(anyw, vmem, vmem, vmem),
         scratch_shapes=[
+            pltpu.VMEM((N, blk, tok), BF16),
+            pltpu.VMEM((N, tok, heads_dev), BF16),
+            pltpu.VMEM((blk, heads_dev), F32),
             pltpu.VMEM((SLOTS, tile, heads_dev), BF16),
             pltpu.VMEM((heads_dev, tok), BF16),
             pltpu.VMEM((T, per, tile, tok), BF16),
@@ -485,6 +538,7 @@
             sem((N // T,)),
             sem((bits, N)),
             sem((N,)),
+            sem((heads_dev // min(512, heads_dev),)),
         ],
         compiler_params=pltpu.CompilerParams(
             collective_id=0, has_side_effects=True, vmem_limit_bytes=60 * 1024 * 1024
@@ -500,7 +554,6 @@
         valid[None, :],
         vsum,
     )
-    grad_out_proj = jnp.dot(exch, attn_all, preferred_element_type=F32)
     loss = (ltot[0, 0] / ctot[0, 0]).reshape(1)
     return (loss, grad_out_proj, qtot[0] * headv, qtot[0] * gain)
 

time: 191 us -> 190 us (level)
  matrix products: 14.5 us -> 0 us
  local copies, waits for them, and re-layouts: 5.66 us -> 13.6 us
  Pallas kernels: 160 us -> 165 us
    dot_general x1 -> x0, matrix products: 14.5 us -> none  [shards(): grad_out_proj = jnp.dot(exch, attn_all, preferred_element_type=F32)]
    unnamed x6 -> x5, local copies, waits for them, and re-layouts: 0.02 us -> 7.89 us
    pallas_call x1, Pallas kernels: 160 us -> 165 us  [shards(): pl.pallas_call(functools.partial(kernel, sizes), out_shape=(jax.ShapeDtyp...]
where the time goes in v3:
time: 190 us
  Pallas kernels  165 us (87%)
  local copies, waits for them, and re-layouts  13.6 us (7%)
  other arithmetic  7.55 us (4%)
  between operations  3.78 us (2%)
    pallas_call x1, Pallas kernels, shards(): pl.pallas_call(functools.partial(kernel, sizes), out_shape=(jax.ShapeDtyp...  165 us
    unnamed x5, local copies, waits for them, and re-layouts  7.89 us

profile of v3, /device:TPU:6, one launch (start us, length us, event | category | flops | bytes accessed | tf_op | source)
XLA Modules:
  0.0 189.7 jit_solution(7506323772457447806)
XLA Ops:
  0.6 0.7 convert_multiply_fusion.1
  1.3 1.3 copy.13.both
  2.7 0.7 convert_element_type.24
  3.3 1.3 convert_divide_fusion.pool
  4.7 0.8 slice_bitcast_fusion.1
  5.4 0.6 convert_subtract_fusion.select
  6.7 1.8 convert_reduce_fusion
  8.5 1.2 convert_bitcast_fusion.valid
  9.6 1.2 broadcast_in_dim.19.vsum
  10.8 0.0 copy-start
  10.8 0.0 copy-start.1
  10.9 164.8 %shard_map.120 = (f32[1024,2048]{1,0:T(8,128)}, f32[1,2048]{1,0:T(1,128)}, f32[8,128]{1,0:T(8,128)}, f32[8,128]{1,0:T(8,128)}) custom-call(bf16[256,2048]{1,0:T(8,128)(2,1)} %attn.1, bf16[8192,2048]{1,0:T(8,128)(2,1)} %weight.1, bf16[256,2048]{1,0:T(8,128)(2,1)} %resid.1, f32[2048,1]{1,0:T(8,128)} %copy.13.both, f32[4,256]{1,0:T(4,128)} %convert_divide_fusion.pool, ...), custom_call_target="tpu_custom_call" | custom-call | tf_op jit(solution)/shard_map/pallas_call | solution.py:495
  175.7 1.2 slice.14
  176.9 1.2 slice.15
  179.4 0.0 copy-done
  179.4 0.0 copy-done.1
  179.4 1.3 convert_multiply_fusion.2
  180.7 7.9 %copy.16 = f32[1024,2048]{1,0:T(8,128)} copy(f32[1024,2048]{1,0:T(8,128)} %get-tuple-element.25) | data formatting | bytes 16777216
  (1 shorter events, 0.0 us)
Async XLA Ops:
  10.8 168.6 %copy-start = (bf16[2048]{0:T(1024)(128)(2,1)S(1)}, bf16[2048]{0:T(1024)(128)(2,1)}, u32[]{:S(2)}) copy-start(bf16[2048]{0:T(1024)(128)(2,1)} %param.13) | copy-start | bytes 12292
  10.8 168.6 %copy-start.1 = (bf16[2048]{0:T(1024)(128)(2,1)S(1)}, bf16[2048]{0:T(1024)(128)(2,1)}, u32[]{:S(2)}) copy-start(bf16[2048]{0:T(1024)(128)(2,1)} %param.12) | copy-start | bytes 12292
